TPU v7x, 128 devices: a whole 4x4x4 slice. The times are simulated.
128 devices in a mesh: section: 4 (over z), dp: 8 (over y, core), mp: 4 (over x).
Axes of the slice: x: 4, y: 4, z: 4, core: 2. Of those that a mesh axis runs over, the one named last changes fastest.
Arguments:
- text: bfloat16 [4, 4096, 4096], P('section', ('dp', 'mp')), may hold values from -6 to 6
- patches: bfloat16 [16384, 1024], P(('section', 'dp')), may hold values from -6 to 6
- segments: int32 [4, 8, 512], P('section', 'dp'), may hold values from 0 to 3, never falling along the last dimension, each value on 1 to 256 neighbouring positions
- loss_mask: int32 [4, 4096], P('section', ('dp', 'mp')), may hold values from 0 to 1, as said below
- tile_batch: int32 [8, 8], P('dp'), may hold values from 0 to 3, as said below
- tile_offset: int32 [8, 8], P('dp'), may hold values from 0 to 448, as said below
- attn_gain: float32 [4, 4096], P('section'), may hold values from 0.5 to 2
- w_query: bfloat16 [4, 4096, 2048], P('section', None, 'mp'), may hold values from -0.09375 to 0.09375
- w_kv: bfloat16 [4, 2, 4096, 512], P('section', None, None, 'mp'), may hold values from -0.09375 to 0.09375
- w_out: bfloat16 [4, 2048, 4096], P('section', 'mp'), may hold values from -0.125 to 0.125
- vis_gain: float32 [2, 1024], replicated, may hold values from 0.5 to 2
- vis_bias: float32 [2, 1024], replicated, may hold values from -3 to 3
- v_qkv: bfloat16 [3, 1024, 1024], P(None, ('section', 'dp'), 'mp'), may hold values from -0.1875 to 0.1875
- v_out: bfloat16 [1024, 1024], P('mp', ('section', 'dp')), may hold values from -0.1875 to 0.1875
- v_up: bfloat16 [1024, 4096], P(('section', 'dp'), 'mp'), may hold values from -0.1875 to 0.1875
- v_down: bfloat16 [4096, 1024], P('mp', ('section', 'dp')), may hold values from -0.09375 to 0.09375
- v_proj: bfloat16 [4096, 4096], P(('section', 'dp'), 'mp'), may hold values from -0.09375 to 0.09375
Outputs:
- hidden: bfloat16 [4, 4096, 4096], P('section', ('dp', 'mp'))
- token_weight: float32 [4, 4096], P('section', ('dp', 'mp'))
Inputs may be any that keep to these rules, and one draw needn't show every extreme that they name: `tile_batch`: in every data-parallel index, the 2 tiles of each section index go 1 to each of two different micro-batches; one micro-batch receives 1 tiles from every section index. `tile_offset`: offsets are multiples of 64; the runs of one sequence never intersect. `loss_mask`: the first position of every sequence is a one.
All inputs are finite; a program needn't handle non-finite values.
Results may differ from a plain program's by a relative error of at most 0.025.
Values may be sent and summed in bfloat16 or wider, within the bound.
A program may use at most 192 MiB of HBM per device.

v0:
```python
import jax
import jax.numpy as jnp
from jax import lax
from jax.sharding import Mesh
from jax.sharding import PartitionSpec as P

HD = 128
VHD = 64
GRID = 16
PATCH = 256
POOL = 64
SECTION_DP = ("section", "dp_0", "dp_1")
SECTION_DP_MP = ("section", "dp_0", "dp_1", "mp")
DP = ("dp_0", "dp_1")
DP_MP = ("dp_0", "dp_1", "mp")
EPS = 1e-05
ROPE_BASE = 500000.0
BLOCKED = -1e30


def copy_for_each(array, axis):
    copies = jnp.broadcast_to(array, (lax.axis_size(axis), *array.shape))
    return lax.all_to_all(copies, axis, split_axis=0, concat_axis=0, tiled=True)


def over_copies(array, axis):
    everything = copy_for_each(array, axis)
    return jnp.sum(everything.astype(jnp.float32), axis=0)


def laid_out(tiles, dim):
    lengths = list(tiles.shape[1:])
    lengths[dim] *= tiles.shape[0]
    return jnp.moveaxis(tiles, 0, dim).reshape(lengths)


def one_gather(arrays, axis, dims):
    flat = jnp.concatenate([a.reshape(-1) for a in arrays])
    lines, at, done = (lax.all_gather(flat, axis), 0, [])
    for a, dim in zip(arrays, dims):
        tiles = lines[:, at : at + a.size].reshape(-1, *a.shape)
        done.append(laid_out(tiles, dim))
        at += a.size
    return tuple(done)


def shifted(value, axis, steps):
    count = lax.axis_size(axis)
    pairs = [(source, (source + steps) % count) for source in range(count)]
    return lax.ppermute(value, axis, pairs)


def over_axes(array, axes):
    for axis in axes:
        array = lax.psum(array, axis)
    return array


def layer_norm(values, gain, bias):
    wide = values.astype(jnp.float32)
    center = wide - jnp.mean(wide, axis=-1, keepdims=True)
    spread = jnp.mean(center * center, axis=-1, keepdims=True)
    return (center * lax.rsqrt(spread + EPS) * gain + bias).astype(jnp.bfloat16)


def rms_norm(values, gain):
    wide = values.astype(jnp.float32)
    power = jnp.mean(wide * wide, axis=-1, keepdims=True)
    return (wide * lax.rsqrt(power + EPS) * gain).astype(jnp.bfloat16)


def rotate(values, positions):
    half_width = values.shape[-1] // 2
    freqs = ROPE_BASE ** (-2.0 * jnp.arange(half_width, dtype=jnp.float32) / values.shape[-1])
    angles = positions.astype(jnp.float32)[:, None] * freqs[None, :]
    cosine = jnp.cos(angles)[:, None, :]
    sinus_part = jnp.sin(angles)[:, None, :]
    first_half = values[..., :half_width]
    second_half = values[..., half_width:]
    return jnp.concatenate(
        [
            first_half * cosine - second_half * sinus_part,
            second_half * cosine + first_half * sinus_part,
        ],
        axis=-1,
    )


def pixel_shuffle(states):
    tile_count = states.shape[0] // PATCH
    side_half = GRID // 2
    width = states.shape[1]
    arranged = states.reshape(tile_count, side_half, 2, side_half, 2, width)
    return arranged.transpose(0, 1, 3, 2, 4, 5).reshape(
        tile_count * side_half * side_half, 4 * width
    )


def block_sum(partial_value):
    return over_copies(partial_value.astype(jnp.bfloat16), "mp").astype(jnp.float32)


def encode_tiles(patches, vis_gain, vis_bias, qkv_full, out_full, up_full, down_full, proj_full):
    tile_count = patches.shape[0] // PATCH
    local_width = qkv_full.shape[2]
    head_count = local_width // VHD
    normed = layer_norm(patches, vis_gain[0], vis_bias[0])
    projected = [
        jnp.dot(normed, qkv_full[index], preferred_element_type=jnp.float32)
        .astype(jnp.bfloat16)
        .reshape(tile_count, PATCH, head_count, VHD)
        for index in range(3)
    ]
    scores = jnp.einsum(
        "tqhd,tkhd->thqk", projected[0], projected[1], preferred_element_type=jnp.float32
    ) * VHD ** (-0.5)
    probs = jax.nn.softmax(scores, axis=-1).astype(jnp.bfloat16)
    mixed = (
        jnp.einsum("thqk,tkhd->tqhd", probs, projected[2], preferred_element_type=jnp.float32)
        .astype(jnp.bfloat16)
        .reshape(tile_count * PATCH, local_width)
    )
    attended = block_sum(jnp.dot(mixed, out_full, preferred_element_type=jnp.float32))
    residual = (patches.astype(jnp.float32) + attended).astype(jnp.bfloat16)
    normed_two = layer_norm(residual, vis_gain[1], vis_bias[1])
    inner = jax.nn.gelu(
        jnp.dot(normed_two, up_full, preferred_element_type=jnp.float32), approximate=False
    ).astype(jnp.bfloat16)
    fed = block_sum(jnp.dot(inner, down_full, preferred_element_type=jnp.float32))
    states = (residual.astype(jnp.float32) + fed).astype(jnp.bfloat16)
    return jnp.dot(pixel_shuffle(states), proj_full, preferred_element_type=jnp.float32).astype(
        jnp.bfloat16
    )


def decoder_layer(active, state, segment_ids, gain, w_query, w_kv, w_out):
    normed = rms_norm(state, gain)
    query_width = w_query.shape[1]
    pair_width = w_kv.shape[2]
    joined_width = query_width + 2 * pair_width
    model_width = w_out.shape[1]
    piece = lax.all_gather(normed, "mp", axis=0, tiled=True)
    row_count = piece.shape[0]

    def project_computed(rows):
        positions = jnp.arange(row_count, dtype=jnp.int32)
        query = jnp.dot(rows, w_query, preferred_element_type=jnp.float32).reshape(
            row_count, query_width // HD, HD
        )
        keyed = jnp.dot(rows, w_kv[0], preferred_element_type=jnp.float32).reshape(
            row_count, pair_width // HD, HD
        )
        valued = jnp.dot(rows, w_kv[1], preferred_element_type=jnp.float32)
        return jnp.concatenate(
            [
                rotate(query, positions).reshape(row_count, query_width),
                rotate(keyed, positions).reshape(row_count, pair_width),
                valued,
            ],
            axis=1,
        ).astype(jnp.bfloat16)

    def project_skipped(rows):
        return jnp.zeros((row_count, joined_width), jnp.bfloat16)

    joined = lax.cond(active, project_computed, project_skipped, piece)
    length = joined.shape[0]
    pair_heads = pair_width // HD
    group_size = query_width // pair_width

    def attend(joined_rows):
        query = joined_rows[:, :query_width].reshape(length, pair_heads, group_size, HD)
        keyed = joined_rows[:, query_width : query_width + pair_width].reshape(
            length, pair_heads, HD
        )
        valued = joined_rows[:, query_width + pair_width :].reshape(length, pair_heads, HD)
        scores = jnp.einsum(
            "qkgd,skd->kgqs", query, keyed, preferred_element_type=jnp.float32
        ) * HD ** (-0.5)
        row_ids = jnp.arange(length, dtype=jnp.int32)
        allowed = (segment_ids[:, None] == segment_ids[None, :]) & (
            row_ids[None, :] <= row_ids[:, None]
        )
        scores = jnp.where(allowed, scores, BLOCKED)
        probs = jax.nn.softmax(scores, axis=-1).astype(jnp.bfloat16)
        return (
            jnp.einsum("kgqs,skd->qkgd", probs, valued, preferred_element_type=jnp.float32)
            .astype(jnp.bfloat16)
            .reshape(length, query_width)
        )

    def attend_skipped(joined_rows):
        return jnp.zeros((length, query_width), jnp.bfloat16)

    mixed = lax.cond(active, attend, attend_skipped, joined)
    count = state.shape[0] * lax.axis_size("mp")

    def out_computed(values):
        return jnp.dot(values, w_out, preferred_element_type=jnp.float32)

    def out_skipped(values):
        return jnp.zeros((count, model_width), jnp.float32)

    summed = lax.psum_scatter(
        lax.cond(active, out_computed, out_skipped, mixed).astype(jnp.bfloat16),
        "mp",
        scatter_dimension=0,
        tiled=True,
    ).astype(jnp.float32)
    updated = (state.astype(jnp.float32) + summed).astype(jnp.bfloat16)
    return jnp.where(active, updated, state)


def shards(
    text,
    patches,
    segments,
    loss_mask,
    tile_batch,
    tile_offset,
    attn_gain,
    w_query,
    w_kv,
    w_out,
    vis_gain,
    vis_bias,
    v_qkv,
    v_out,
    v_up,
    v_down,
    v_proj,
):
    sections = lax.axis_size("section")
    section_at = lax.axis_index("section")
    part_at = lax.axis_index("mp")
    qkv_full, out_full, up_full, down_full, proj_full = one_gather(
        (v_qkv, v_out, v_up, v_down, v_proj), SECTION_DP, (1, 1, 0, 1, 0)
    )
    embedded = encode_tiles(
        patches, vis_gain, vis_bias, qkv_full, out_full, up_full, down_full, proj_full
    )
    length = segments.shape[2]
    tiles_here = embedded.shape[0] // POOL
    batch_all = tile_batch[0]
    offset_all = tile_offset[0]
    own_batch = lax.dynamic_slice_in_dim(batch_all, section_at * tiles_here, tiles_here, 0)
    capacity = tiles_here // 2
    block_rows = capacity * POOL
    local_ids = jnp.arange(tiles_here, dtype=jnp.int32)
    local_same = (own_batch[:, None] == own_batch[None, :]) & (
        local_ids[None, :] < local_ids[:, None]
    )
    local_rank = jnp.sum(local_same.astype(jnp.int32), axis=1)
    send_rows = jnp.arange(sections * block_rows, dtype=jnp.int32)
    send_target = send_rows // block_rows
    send_rank = send_rows % block_rows // POOL
    send_match = (own_batch[None, :] == send_target[:, None]) & (
        local_rank[None, :] == send_rank[:, None]
    )
    own_rows = jnp.arange(tiles_here * POOL, dtype=jnp.int32)
    send_pick = jnp.repeat(send_match, POOL, axis=1) & (
        (own_rows % POOL)[None, :] == (send_rows % POOL)[:, None]
    )
    blocks = jnp.dot(
        send_pick.astype(jnp.bfloat16), embedded, preferred_element_type=jnp.float32
    ).astype(jnp.bfloat16)
    arrived = lax.all_to_all(blocks, "section", split_axis=0, concat_axis=0, tiled=True)
    tile_ids = jnp.arange(batch_all.shape[0], dtype=jnp.int32)
    source_ids = tile_ids // tiles_here
    tile_same = (
        (batch_all[:, None] == batch_all[None, :])
        & (source_ids[:, None] == source_ids[None, :])
        & (tile_ids[None, :] < tile_ids[:, None])
    )
    tile_rank = jnp.sum(tile_same.astype(jnp.int32), axis=1)
    slot_rows = jnp.arange(sections * block_rows, dtype=jnp.int32)
    slot_source = slot_rows // block_rows
    slot_rank = slot_rows % block_rows // POOL
    match = (
        (batch_all[None, :] == section_at)
        & (source_ids[None, :] == slot_source[:, None])
        & (tile_rank[None, :] == slot_rank[:, None])
    )
    slot_place = jnp.sum(match.astype(jnp.int32) * offset_all[None, :], axis=1) + slot_rows % POOL
    slot_valid = jnp.any(match, axis=1)
    places = jnp.arange(length, dtype=jnp.int32)
    picker = ((places[:, None] == slot_place[None, :]) & slot_valid[None, :]).astype(jnp.bfloat16)
    image_cols = jnp.dot(picker, arrived, preferred_element_type=jnp.float32).astype(jnp.bfloat16)
    image_rows = lax.all_to_all(image_cols, "mp", split_axis=0, concat_axis=1, tiled=True)
    shard_rows = image_rows.shape[0]
    positions = part_at * shard_rows + jnp.arange(shard_rows, dtype=jnp.int32)
    covered = jnp.any(
        (batch_all[None, :] == section_at)
        & (positions[:, None] >= offset_all[None, :])
        & (positions[:, None] < offset_all[None, :] + POOL),
        axis=1,
    )
    start_state = jnp.where(covered[:, None], image_rows, text[0])
    gain_here = attn_gain[0]
    query_here = w_query[0]
    pair_here = w_kv[0]
    out_here = w_out[0]
    state = start_state
    segment_ids = segments[0, 0]
    for tick_index in range(2 * sections):
        if tick_index < 2 * sections - 1:
            micro_at = jnp.mod(section_at - tick_index, sections)
            begin_at = jnp.mod(sections - micro_at, sections)
            active = (tick_index >= begin_at) & (tick_index < begin_at + sections)
            state = decoder_layer(
                active, state, segment_ids, gain_here, query_here, pair_here, out_here
            )
        state, segment_ids = shifted((state, segment_ids), "section", 1)
    totals = over_axes(jnp.sum(loss_mask), SECTION_DP_MP)
    scaling = float(sections * lax.axis_size(DP) * length)
    token_weight = loss_mask.astype(jnp.float32) * scaling / totals.astype(jnp.float32)
    return (state[None], token_weight)


def solution(mesh):
    split = Mesh(
        mesh.devices.reshape(mesh.shape["section"], 4, 2, mesh.shape["mp"]),
        ("section", "dp_0", "dp_1", "mp"),
    )
    return jax.shard_map(
        shards,
        mesh=split,
        in_specs=(
            P("section", DP_MP, None),
            P(SECTION_DP, None),
            P("section", DP, None),
            P("section", DP_MP),
            P(DP, None),
            P(DP, None),
            P("section", None),
            P("section", None, "mp"),
            P("section", None, None, "mp"),
            P("section", "mp", None),
            P(),
            P(),
            P(None, SECTION_DP, "mp"),
            P("mp", SECTION_DP),
            P(SECTION_DP, "mp"),
            P("mp", SECTION_DP),
            P(SECTION_DP, "mp"),
        ),
        out_specs=(P("section", DP_MP, None), P("section", DP_MP)),
        check_vma=False,
    )
```

profile of v0, /device:TPU:32, one launch (start us, length us, event | category | flops | bytes accessed | tf_op | source)
XLA Modules:
  0.0 1387.6 jit_solution(4361427265575410445)
XLA Ops:
  16.4 66.2 %all-gather.24.cloned.1.call-done = bf16[7340032]{0:T(1024)(128)(2,1)} async-done(((bf16[229376]{0:T(1024)(128)(2,1)}), bf16[7340032]{0:T(1024)(128)(2,1)}) %all-gather.24.cloned.1.call-update) | async-done | bytes 14680080 | tf_op jit(solution)/shard_map/all_gather | solution.py:39
  82.6 13.2 reshape.1320
  122.5 8.0 reshape.1316
  130.5 8.2 copy.206
  141.0 27.2 %all-to-all-done = bf16[4,512,1024]{2,1,0:T(8,128)(2,1)} async-done(((bf16[4,512,1024]{2,1,0:T(8,128)(2,1)}), bf16[4,512,1024]{2,1,0:T(8,128)(2,1)}, u32[]{:S(2)}, u32[]{:S(2)}) %all-to-all-start) | async-done | bytes 4194336 | tf_op jit(solution)/shard_map/all_to_all | solution.py:23
  172.4 8.5 convolution_convert_fusion.8
  189.6 7.2 slice.282
  196.8 9.0 reshape_reshape.7
  205.8 31.9 %all-to-all-done.1 = bf16[4,512,1024]{2,1,0:T(8,128)(2,1)} async-done(((bf16[4,512,1024]{2,1,0:T(8,128)(2,1)}), bf16[4,512,1024]{2,1,0:T(8,128)(2,1)}, u32[]{:S(2)}, u32[]{:S(2)}) %all-to-all-start.1) | async-done | bytes 4194336 | tf_op jit(solution)/shard_map/all_to_all | solution.py:23
  268.5 11.0 all-to-all-done.3
  285.6 46.9 %all-gather.10.cloned.1.call-done = bf16[512,4096]{1,0:T(8,128)(2,1)} async-done(((bf16[128,4096]{1,0:T(8,128)(2,1)}), bf16[512,4096]{1,0:T(8,128)(2,1)}) %all-gather.10.cloned.1.call-update) | async-done | bytes 4194320 | tf_op jit(solution)/shard_map/all_gather | solution.py:142
  341.9 62.8 %reduce-scatter.8.cloned.1.call-done = bf16[128,4096]{1,0:T(8,128)(2,1)} async-done(((bf16[512,4096]{1,0:T(8,128)(2,1)}), bf16[128,4096]{1,0:T(8,128)(2,1)}) %reduce-scatter.8.cloned.1.call-update) | async-done | bytes 1048592 | tf_op jit(solution)/shard_map/reduce_scatter | solution.py:204
  408.5 23.3 %collective-permute-done = bf16[128,4096]{1,0:T(8,128)(2,1)S(1)} collective-permute-done((bf16[128,4096]{1,0:T(8,128)(2,1)S(1)}, bf16[128,4096]{1,0:T(8,128)(2,1)S(1)}, u32[]{:S(2)}, u32[]{:S(2)}) %collective-permute-start) | collective-permute-done | bytes 1048608 | tf_op jit(solution)/shard_map/ppermute | solution.py:50
  435.0 46.4 %all-gather.12.cloned.1.call-done = bf16[512,4096]{1,0:T(8,128)(2,1)} async-done(((bf16[128,4096]{1,0:T(8,128)(2,1)}), bf16[512,4096]{1,0:T(8,128)(2,1)}) %all-gather.12.cloned.1.call-update) | async-done | bytes 4194320 | tf_op jit(solution)/shard_map/all_gather | solution.py:142
  481.4 10.1 conditional.24
  491.6 10.4 conditional.25
  502.0 7.1 conditional.26
  502.4 6.7 fusion.357
  509.2 45.7 %reduce-scatter.10.cloned.1.call-done = bf16[128,4096]{1,0:T(8,128)(2,1)} async-done(((bf16[512,4096]{1,0:T(8,128)(2,1)}), bf16[128,4096]{1,0:T(8,128)(2,1)}) %reduce-scatter.10.cloned.1.call-update) | async-done | bytes 1048592 | tf_op jit(solution)/shard_map/reduce_scatter | solution.py:204
  558.0 23.3 %collective-permute-done.2 = bf16[128,4096]{1,0:T(8,128)(2,1)S(1)} collective-permute-done((bf16[128,4096]{1,0:T(8,128)(2,1)S(1)}, bf16[128,4096]{1,0:T(8,128)(2,1)S(1)}, u32[]{:S(2)}, u32[]{:S(2)}) %collective-permute-start.2) | collective-permute-done | bytes 1048608 | tf_op jit(solution)/shard_map/ppermute | solution.py:50
  584.6 46.4 %all-gather.14.cloned.1.call-done = bf16[512,4096]{1,0:T(8,128)(2,1)} async-done(((bf16[128,4096]{1,0:T(8,128)(2,1)}), bf16[512,4096]{1,0:T(8,128)(2,1)}) %all-gather.14.cloned.1.call-update) | async-done | bytes 4194320 | tf_op jit(solution)/shard_map/all_gather | solution.py:142
  631.0 10.1 conditional.27
  641.2 10.6 conditional.28
  651.8 6.7 conditional.29
  658.6 47.3 %reduce-scatter.12.cloned.1.call-done = bf16[128,4096]{1,0:T(8,128)(2,1)} async-done(((bf16[512,4096]{1,0:T(8,128)(2,1)}), bf16[128,4096]{1,0:T(8,128)(2,1)}) %reduce-scatter.12.cloned.1.call-update) | async-done | bytes 1048592 | tf_op jit(solution)/shard_map/reduce_scatter | solution.py:204
  709.0 23.3 %collective-permute-done.4 = bf16[128,4096]{1,0:T(8,128)(2,1)S(1)} collective-permute-done((bf16[128,4096]{1,0:T(8,128)(2,1)S(1)}, bf16[128,4096]{1,0:T(8,128)(2,1)S(1)}, u32[]{:S(2)}, u32[]{:S(2)}) %collective-permute-start.4) | collective-permute-done | bytes 1048608 | tf_op jit(solution)/shard_map/ppermute | solution.py:50
  735.6 46.4 %all-gather.16.cloned.1.call-done = bf16[512,4096]{1,0:T(8,128)(2,1)} async-done(((bf16[128,4096]{1,0:T(8,128)(2,1)}), bf16[512,4096]{1,0:T(8,128)(2,1)}) %all-gather.16.cloned.1.call-update) | async-done | bytes 4194320 | tf_op jit(solution)/shard_map/all_gather | solution.py:142
  782.0 10.4 conditional.30
  792.3 10.5 conditional.31
  802.8 6.7 conditional.32
  810.0 46.8 %reduce-scatter.14.cloned.1.call-done = bf16[128,4096]{1,0:T(8,128)(2,1)} async-done(((bf16[512,4096]{1,0:T(8,128)(2,1)}), bf16[128,4096]{1,0:T(8,128)(2,1)}) %reduce-scatter.14.cloned.1.call-update) | async-done | bytes 1048592 | tf_op jit(solution)/shard_map/reduce_scatter | solution.py:204
  860.0 23.3 %collective-permute-done.6 = bf16[128,4096]{1,0:T(8,128)(2,1)S(1)} collective-permute-done((bf16[128,4096]{1,0:T(8,128)(2,1)S(1)}, bf16[128,4096]{1,0:T(8,128)(2,1)S(1)}, u32[]{:S(2)}, u32[]{:S(2)}) %collective-permute-start.6) | collective-permute-done | bytes 1048608 | tf_op jit(solution)/shard_map/ppermute | solution.py:50
  886.6 46.4 %all-gather.18.cloned.1.call-done = bf16[512,4096]{1,0:T(8,128)(2,1)} async-done(((bf16[128,4096]{1,0:T(8,128)(2,1)}), bf16[512,4096]{1,0:T(8,128)(2,1)}) %all-gather.18.cloned.1.call-update) | async-done | bytes 4194320 | tf_op jit(solution)/shard_map/all_gather | solution.py:142
  933.0 10.2 conditional.33
  943.1 10.5 conditional.34
  953.6 6.9 conditional.35
  953.8 6.7 fusion.360
  960.5 47.3 %reduce-scatter.16.cloned.1.call-done = bf16[128,4096]{1,0:T(8,128)(2,1)} async-done(((bf16[512,4096]{1,0:T(8,128)(2,1)}), bf16[128,4096]{1,0:T(8,128)(2,1)}) %reduce-scatter.16.cloned.1.call-update) | async-done | bytes 1048592 | tf_op jit(solution)/shard_map/reduce_scatter | solution.py:204
  1011.0 23.3 %collective-permute-done.8 = bf16[128,4096]{1,0:T(8,128)(2,1)S(1)} collective-permute-done((bf16[128,4096]{1,0:T(8,128)(2,1)S(1)}, bf16[128,4096]{1,0:T(8,128)(2,1)S(1)}, u32[]{:S(2)}, u32[]{:S(2)}) %collective-permute-start.8) | collective-permute-done | bytes 1048608 | tf_op jit(solution)/shard_map/ppermute | solution.py:50
  1037.5 46.4 %all-gather.20.cloned.1.call-done = bf16[512,4096]{1,0:T(8,128)(2,1)} async-done(((bf16[128,4096]{1,0:T(8,128)(2,1)}), bf16[512,4096]{1,0:T(8,128)(2,1)}) %all-gather.20.cloned.1.call-update) | async-done | bytes 4194320 | tf_op jit(solution)/shard_map/all_gather | solution.py:142
  1088.5 70.3 %reduce-scatter.18.cloned.1.call-done = bf16[128,4096]{1,0:T(8,128)(2,1)} async-done(((bf16[512,4096]{1,0:T(8,128)(2,1)}), bf16[128,4096]{1,0:T(8,128)(2,1)}) %reduce-scatter.18.cloned.1.call-update) | async-done | bytes 1048592 | tf_op jit(solution)/shard_map/reduce_scatter | solution.py:204
  1161.9 23.3 %collective-permute-done.10 = bf16[128,4096]{1,0:T(8,128)(2,1)S(1)} collective-permute-done((bf16[128,4096]{1,0:T(8,128)(2,1)S(1)}, bf16[128,4096]{1,0:T(8,128)(2,1)S(1)}, u32[]{:S(2)}, u32[]{:S(2)}) %collective-permute-start.10) | collective-permute-done | bytes 1048608 | tf_op jit(solution)/shard_map/ppermute | solution.py:50
  1188.5 46.4 %all-gather.22.cloned.1.call-done = bf16[512,4096]{1,0:T(8,128)(2,1)} async-done(((bf16[128,4096]{1,0:T(8,128)(2,1)}), bf16[512,4096]{1,0:T(8,128)(2,1)}) %all-gather.22.cloned.1.call-update) | async-done | bytes 4194320 | tf_op jit(solution)/shard_map/all_gather | solution.py:142
  1237.8 65.9 %reduce-scatter.20.cloned.1.call-done = bf16[128,4096]{1,0:T(8,128)(2,1)} async-done(((bf16[512,4096]{1,0:T(8,128)(2,1)}), bf16[128,4096]{1,0:T(8,128)(2,1)}) %reduce-scatter.20.cloned.1.call-update) | async-done | bytes 1048592 | tf_op jit(solution)/shard_map/reduce_scatter | solution.py:204
  1306.9 23.3 %collective-permute-done.12 = bf16[128,4096]{1,0:T(8,128)(2,1)S(1)} collective-permute-done((bf16[128,4096]{1,0:T(8,128)(2,1)S(1)}, bf16[128,4096]{1,0:T(8,128)(2,1)S(1)}, u32[]{:S(2)}, u32[]{:S(2)}) %collective-permute-start.12) | collective-permute-done | bytes 1048608 | tf_op jit(solution)/shard_map/ppermute | solution.py:50
  1332.3 26.3 %psum.28 = s32[]{:T(128)} all-reduce(s32[]{:T(128)} %reduce_sum.242), channel_id=1, replica_groups=mesh['section'=4,'dp_0'=4,'dp_1'=2,'mp'=4] {'section'}, use_global_device_ids=true, to_apply=%region_84.85 | all-reduce | flops 1 | bytes 8 | tf_op jit(solution)/shard_map/psum | solution.py:55
  1358.6 9.5 psum.29
  1370.6 7.9 psum.31
  (294 shorter events, 260.1 us)
Async XLA Ops:
  7.2 7.3 copy-start.8
  7.2 7.7 copy-start.17
  7.2 7.7 copy-start.18
  7.2 75.4 %all-gather.24.cloned.1.call-start = ((), (), s32[]{:S(2)}) async-start(), calls=%async_computation.25 | async-start | bytes 15138816 | tf_op jit(solution)/shard_map/all_gather | solution.py:39
  95.8 2.7 copy-start.12
  113.6 54.6 %all-to-all-start = ((bf16[4,512,1024]{2,1,0:T(8,128)(2,1)}), bf16[4,512,1024]{2,1,0:T(8,128)(2,1)}, u32[]{:S(2)}, u32[]{:S(2)}) async-start(bf16[4,512,1024]{2,1,0:T(8,128)(2,1)} %broadcast_in_dim.76), calls=%async_computation | async-start | bytes 8388608 | tf_op jit(solution)/shard_map/all_to_all | solution.py:23
  130.5 8.2 copy-start.11
  183.6 5.4 copy-start.20
  183.6 54.1 %all-to-all-start.1 = ((bf16[4,512,1024]{2,1,0:T(8,128)(2,1)}), bf16[4,512,1024]{2,1,0:T(8,128)(2,1)}, u32[]{:S(2)}, u32[]{:S(2)}) async-start(bf16[4,512,1024]{2,1,0:T(8,128)(2,1)} %broadcast_in_dim.85), calls=%async_computation.1 | async-start | bytes 8388608 | tf_op jit(solution)/shard_map/all_to_all | solution.py:23
  243.6 10.8 copy-start.19
  249.2 17.6 %copy-start.9 = (bf16[1,128,4096]{2,1,0:T(8,128)(2,1)S(1)}, bf16[1,128,4096]{2,1,0:T(8,128)(2,1)}, u32[]{:S(2)}) copy-start(bf16[1,128,4096]{2,1,0:T(8,128)(2,1)} %param.59) | copy-start | bytes 3145732
  249.3 11.7 all-to-all-start.2
  262.4 21.6 %copy-start.14 = (f32[1,4096]{1,0:T(1,128)S(1)}, f32[1,4096]{1,0:T(1,128)}, u32[]{:S(2)}) copy-start(f32[1,4096]{1,0:T(1,128)} %param.65) | copy-start | bytes 49156
  262.4 17.1 %all-to-all-start.3 = ((bf16[4,128,1024]{2,1,0:T(8,128)(2,1)}), bf16[4,128,1024]{2,1,0:T(8,128)(2,1)}, u32[]{:S(2)}, u32[]{:S(2)}) async-start(bf16[4,128,1024]{2,1,0:T(8,128)(2,1)} %bitcast.135), calls=%async_computation.3 | async-start | bytes 2097152 | tf_op jit(solution)/shard_map/all_to_all | solution.py:289
  266.8 65.7 %all-gather.10.cloned.1.call-start = ((), (), s32[]{:S(2)}) async-start(), calls=%async_computation.11 | async-start | bytes 5242880 | tf_op jit(solution)/shard_map/all_gather | solution.py:142
  268.5 63.9 %copy-start = (bf16[1,2,4096,128]{3,2,1,0:T(8,128)(2,1)S(1)}, bf16[1,2,4096,128]{3,2,1,0:T(8,128)(2,1)}, u32[]{:S(2)}) copy-start(bf16[1,2,4096,128]{3,2,1,0:T(8,128)(2,1)} %param.67) | copy-start | bytes 6291460
  285.5 119.2 %reduce-scatter.8.cloned.1.call-start = ((), (), s32[]{:S(2)}) async-start(), calls=%async_computation.12 | async-start | bytes 5242880 | tf_op jit(solution)/shard_map/reduce_scatter | solution.py:204
  336.9 144.5 %all-gather.12.cloned.1.call-start = ((), (), s32[]{:S(2)}) async-start(), calls=%async_computation.13 | async-start | bytes 5242880 | tf_op jit(solution)/shard_map/all_gather | solution.py:142
  406.8 24.9 %collective-permute-start = (bf16[128,4096]{1,0:T(8,128)(2,1)S(1)}, bf16[128,4096]{1,0:T(8,128)(2,1)S(1)}, u32[]{:S(2)}, u32[]{:S(2)}) collective-permute-start(bf16[128,4096]{1,0:T(8,128)(2,1)S(1)} %fusion.241), channel_id=1, source_target_pairs={{0,32},{32,64},{64,96},{96,0},{1,33},{33,65},{65,97},{97,1},{2,34}... | collective-permute-start | bytes 3145736 | tf_op jit(solution)/shard_map/ppermute | solution.py:50
  433.4 121.5 %reduce-scatter.10.cloned.1.call-start = ((), (), s32[]{:S(2)}) async-start(), calls=%async_computation.14 | async-start | bytes 5242880 | tf_op jit(solution)/shard_map/reduce_scatter | solution.py:204
  433.4 58.2 %collective-permute-start.1 = (s32[512]{0:T(512)S(1)}, s32[512]{0:T(512)S(1)}, u32[]{:S(2)}, u32[]{:S(2)}) collective-permute-start(s32[512]{0:T(512)S(1)} %bitcast.536), channel_id=1, source_target_pairs={{0,32},{32,64},{64,96},{96,0},{1,33},{33,65},{65,97},{97,1},{2,34}... | collective-permute-start | bytes 6152 | tf_op jit(solution)/shard_map/ppermute | solution.py:50
  481.4 3.9 copy-start.2
  509.2 121.9 %all-gather.14.cloned.1.call-start = ((), (), s32[]{:S(2)}) async-start(), calls=%async_computation.15 | async-start | bytes 5242880 | tf_op jit(solution)/shard_map/all_gather | solution.py:142
  556.4 24.9 %collective-permute-start.2 = (bf16[128,4096]{1,0:T(8,128)(2,1)S(1)}, bf16[128,4096]{1,0:T(8,128)(2,1)S(1)}, u32[]{:S(2)}, u32[]{:S(2)}) collective-permute-start(bf16[128,4096]{1,0:T(8,128)(2,1)S(1)} %fusion.240), channel_id=1, source_target_pairs={{0,32},{32,64},{64,96},{96,0},{1,33},{33,65},{65,97},{97,1},{2,34}... | collective-permute-start | bytes 3145736 | tf_op jit(solution)/shard_map/ppermute | solution.py:50
  583.0 122.9 %reduce-scatter.12.cloned.1.call-start = ((), (), s32[]{:S(2)}) async-start(), calls=%async_computation.16 | async-start | bytes 5242880 | tf_op jit(solution)/shard_map/reduce_scatter | solution.py:204
  583.0 58.2 %collective-permute-start.3 = (s32[512]{0:T(512)S(1)}, s32[512]{0:T(512)S(1)}, u32[]{:S(2)}, u32[]{:S(2)}) collective-permute-start(s32[512]{0:T(512)S(1)} %collective-permute-done.1), channel_id=1, source_target_pairs={{0,32},{32,64},{64,96},{96,0},{1,33},{33,65},{65,97},{97,1},{2,34}... | collective-permute-start | bytes 6152 | tf_op jit(solution)/shard_map/ppermute | solution.py:50
  631.0 3.9 copy-start.3
  658.5 123.4 %all-gather.16.cloned.1.call-start = ((), (), s32[]{:S(2)}) async-start(), calls=%async_computation.17 | async-start | bytes 5242880 | tf_op jit(solution)/shard_map/all_gather | solution.py:142
  707.3 24.9 %collective-permute-start.4 = (bf16[128,4096]{1,0:T(8,128)(2,1)S(1)}, bf16[128,4096]{1,0:T(8,128)(2,1)S(1)}, u32[]{:S(2)}, u32[]{:S(2)}) collective-permute-start(bf16[128,4096]{1,0:T(8,128)(2,1)S(1)} %fusion.239), channel_id=1, source_target_pairs={{0,32},{32,64},{64,96},{96,0},{1,33},{33,65},{65,97},{97,1},{2,34}... | collective-permute-start | bytes 3145736 | tf_op jit(solution)/shard_map/ppermute | solution.py:50
  733.9 122.9 %reduce-scatter.14.cloned.1.call-start = ((), (), s32[]{:S(2)}) async-start(), calls=%async_computation.18 | async-start | bytes 5242880 | tf_op jit(solution)/shard_map/reduce_scatter | solution.py:204
  733.9 58.4 %collective-permute-start.5 = (s32[512]{0:T(512)S(1)}, s32[512]{0:T(512)S(1)}, u32[]{:S(2)}, u32[]{:S(2)}) collective-permute-start(s32[512]{0:T(512)S(1)} %collective-permute-done.3), channel_id=1, source_target_pairs={{0,32},{32,64},{64,96},{96,0},{1,33},{33,65},{65,97},{97,1},{2,34}... | collective-permute-start | bytes 6152 | tf_op jit(solution)/shard_map/ppermute | solution.py:50
  782.1 3.9 copy-start.5
  809.5 123.4 %all-gather.18.cloned.1.call-start = ((), (), s32[]{:S(2)}) async-start(), calls=%async_computation.19 | async-start | bytes 5242880 | tf_op jit(solution)/shard_map/all_gather | solution.py:142
  858.4 24.9 %collective-permute-start.6 = (bf16[128,4096]{1,0:T(8,128)(2,1)S(1)}, bf16[128,4096]{1,0:T(8,128)(2,1)S(1)}, u32[]{:S(2)}, u32[]{:S(2)}) collective-permute-start(bf16[128,4096]{1,0:T(8,128)(2,1)S(1)} %fusion.238), channel_id=1, source_target_pairs={{0,32},{32,64},{64,96},{96,0},{1,33},{33,65},{65,97},{97,1},{2,34}... | collective-permute-start | bytes 3145736 | tf_op jit(solution)/shard_map/ppermute | solution.py:50
  884.9 122.9 %reduce-scatter.16.cloned.1.call-start = ((), (), s32[]{:S(2)}) async-start(), calls=%async_computation.20 | async-start | bytes 5242880 | tf_op jit(solution)/shard_map/reduce_scatter | solution.py:204
  884.9 58.2 %collective-permute-start.7 = (s32[512]{0:T(512)S(1)}, s32[512]{0:T(512)S(1)}, u32[]{:S(2)}, u32[]{:S(2)}) collective-permute-start(s32[512]{0:T(512)S(1)} %collective-permute-done.5), channel_id=1, source_target_pairs={{0,32},{32,64},{64,96},{96,0},{1,33},{33,65},{65,97},{97,1},{2,34}... | collective-permute-start | bytes 6152 | tf_op jit(solution)/shard_map/ppermute | solution.py:50
  933.0 3.9 copy-start.6
  960.5 123.4 %all-gather.20.cloned.1.call-start = ((), (), s32[]{:S(2)}) async-start(), calls=%async_computation.21 | async-start | bytes 5242880 | tf_op jit(solution)/shard_map/all_gather | solution.py:142
  1009.3 24.9 %collective-permute-start.8 = (bf16[128,4096]{1,0:T(8,128)(2,1)S(1)}, bf16[128,4096]{1,0:T(8,128)(2,1)S(1)}, u32[]{:S(2)}, u32[]{:S(2)}) collective-permute-start(bf16[128,4096]{1,0:T(8,128)(2,1)S(1)} %fusion.237), channel_id=1, source_target_pairs={{0,32},{32,64},{64,96},{96,0},{1,33},{33,65},{65,97},{97,1},{2,34}... | collective-permute-start | bytes 3145736 | tf_op jit(solution)/shard_map/ppermute | solution.py:50
  1035.9 122.9 %reduce-scatter.18.cloned.1.call-start = ((), (), s32[]{:S(2)}) async-start(), calls=%async_computation.22 | async-start | bytes 5242880 | tf_op jit(solution)/shard_map/reduce_scatter | solution.py:204
  1035.9 48.9 %collective-permute-start.9 = (s32[512]{0:T(512)S(1)}, s32[512]{0:T(512)S(1)}, u32[]{:S(2)}, u32[]{:S(2)}) collective-permute-start(s32[512]{0:T(512)S(1)} %collective-permute-done.7), channel_id=1, source_target_pairs={{0,32},{32,64},{64,96},{96,0},{1,33},{33,65},{65,97},{97,1},{2,34}... | collective-permute-start | bytes 6152 | tf_op jit(solution)/shard_map/ppermute | solution.py:50
  1088.4 146.5 %all-gather.22.cloned.1.call-start = ((), (), s32[]{:S(2)}) async-start(), calls=%async_computation.23 | async-start | bytes 5242880 | tf_op jit(solution)/shard_map/all_gather | solution.py:142
  1160.3 24.9 %collective-permute-start.10 = (bf16[128,4096]{1,0:T(8,128)(2,1)S(1)}, bf16[128,4096]{1,0:T(8,128)(2,1)S(1)}, u32[]{:S(2)}, u32[]{:S(2)}) collective-permute-start(bf16[128,4096]{1,0:T(8,128)(2,1)S(1)} %fusion.236), channel_id=1, source_target_pairs={{0,32},{32,64},{64,96},{96,0},{1,33},{33,65},{65,97},{97,1},{2,34}... | collective-permute-start | bytes 3145736 | tf_op jit(solution)/shard_map/ppermute | solution.py:50
  1186.8 116.9 %reduce-scatter.20.cloned.1.call-start = ((), (), s32[]{:S(2)}) async-start(), calls=%async_computation.24 | async-start | bytes 5242880 | tf_op jit(solution)/shard_map/reduce_scatter | solution.py:204
  1186.9 48.3 %collective-permute-start.11 = (s32[512]{0:T(512)S(1)}, s32[512]{0:T(512)S(1)}, u32[]{:S(2)}, u32[]{:S(2)}) collective-permute-start(s32[512]{0:T(512)S(1)} %collective-permute-done.9), channel_id=1, source_target_pairs={{0,32},{32,64},{64,96},{96,0},{1,33},{33,65},{65,97},{97,1},{2,34}... | collective-permute-start | bytes 6152 | tf_op jit(solution)/shard_map/ppermute | solution.py:50
  1237.8 93.9 %copy-start.28 = (s32[1,128]{1,0:T(1,128)S(1)}, s32[1,128]{1,0:T(1,128)}, u32[]{:S(2)}) copy-start(s32[1,128]{1,0:T(1,128)} %param.62) | copy-start | bytes 1540
  1305.3 24.9 %collective-permute-start.12 = (bf16[128,4096]{1,0:T(8,128)(2,1)S(1)}, bf16[128,4096]{1,0:T(8,128)(2,1)S(1)}, u32[]{:S(2)}, u32[]{:S(2)}) collective-permute-start(bf16[128,4096]{1,0:T(8,128)(2,1)S(1)} %fusion.235), channel_id=1, source_target_pairs={{0,32},{32,64},{64,96},{96,0},{1,33},{33,65},{65,97},{97,1},{2,34}... | collective-permute-start | bytes 3145736 | tf_op jit(solution)/shard_map/ppermute | solution.py:50
  1330.1 49.6 %collective-permute-start.13 = (bf16[128,4096]{1,0:T(8,128)(2,1)S(1)}, bf16[128,4096]{1,0:T(8,128)(2,1)S(1)}, u32[]{:S(2)}, u32[]{:S(2)}) collective-permute-start(bf16[128,4096]{1,0:T(8,128)(2,1)S(1)} %collective-permute-done.12), channel_id=1, source_target_pairs={{0,32},{32,64},{64,96},{96,0},{1,33},{33,65},{65,97},{97,1},{2,34}... | collective-permute-start | bytes 3145736 | tf_op jit(solution)/shard_map/ppermute | solution.py:50
  (10 other events, 17.0 us)
Sparse Core Ops, SparseCore 0:
  13.2 69.3 all-gather.23
  285.6 46.8 all-gather.9
  337.1 67.6 reduce-scatter.7
  433.5 47.9 all-gather.11
  509.3 45.5 reduce-scatter.9
  583.1 47.8 all-gather.13
  658.6 47.1 reduce-scatter.11
  734.0 47.8 all-gather.15
  809.6 47.1 reduce-scatter.13
  885.0 47.9 all-gather.17
  960.6 47.1 reduce-scatter.15
  1036.0 47.8 all-gather.19
  1088.5 70.1 reduce-scatter.17
  1187.0 47.8 all-gather.21
  1237.9 65.7 reduce-scatter.19
where the time goes:
time: 1400 us; the launch traced here: 1390 us
  waiting for transfers between devices  1020 us (73%)
  local copies, waits for them, and re-layouts  106 us (8%)
  matrix products  101 us (7%)
  other arithmetic  51.4 us (4%)
  starting transfers between devices  48.4 us (3%)
  blocking collectives  46.2 us (3%)
  between operations  15.6 us (1%)
    reduce_scatter x7, waiting for transfers between devices, decoder_layer(): lax.psum_scatter(lax.cond(active, out_computed, out_skipped, mixed).astyp...  386 us
    all_gather x7, waiting for transfers between devices, decoder_layer(): piece = lax.all_gather(normed, 'mp', axis=0, tiled=True)  325 us
    ppermute x14, waiting for transfers between devices, shifted(): return lax.ppermute(value, axis, pairs)  163 us
    all_gather x1, waiting for transfers between devices, one_gather(): lines, at, done = (lax.all_gather(flat, axis), 0, [])  66.2 us
    all_to_all x2, waiting for transfers between devices, copy_for_each(): return lax.all_to_all(copies, axis, split_axis=0, concat_axis=0, tiled=True)  59.1 us
    psum x4, blocking collectives, over_axes(): array = lax.psum(array, axis)  46.2 us
  transfers between devices with their start and end apart: 33, of which 26 were waited for; matrix products, arithmetic and copies ran while one was open for 6% of the time, Pallas kernels for 0%

commit v1 on v0

--- a/solution.py
+++ b/solution.py
@@ -16,6 +16,14 @@
 EPS = 1e-05
 ROPE_BASE = 500000.0
 BLOCKED = -1e30
+
+
+def gather_from_all(shard, axis, dim):
+    size = lax.axis_size(axis)
+    repeats = [size if d == dim else 1 for d in range(shard.ndim)]
+    return lax.all_to_all(
+        jnp.tile(shard, repeats), axis, split_axis=dim, concat_axis=dim, tiled=True
+    )
 
 
 def copy_for_each(array, axis):
@@ -139,7 +147,7 @@
     pair_width = w_kv.shape[2]
     joined_width = query_width + 2 * pair_width
     model_width = w_out.shape[1]
-    piece = lax.all_gather(normed, "mp", axis=0, tiled=True)
+    piece = gather_from_all(normed, "mp", 0)
     row_count = piece.shape[0]
 
     def project_computed(rows):

time: 1400 us -> 1460 us (1.043)
  starting transfers between devices: 48.4 us -> 76.8 us
  local copies, waits for them, and re-layouts: 106 us -> 127 us
  matrix products: 101 us -> 119 us
    all_gather x7 -> x0, waiting for transfers between devices: 325 us -> none  [decoder_layer(): piece = lax.all_gather(normed, 'mp', axis=0, tiled=True)]
    all_to_all x0 -> x7, waiting for transfers between devices: none -> 318 us  [gather_from_all(): lax.all_to_all(jnp.tile(shard, repeats), axis, split_axis=dim, concat_axi...]
    all_to_all x0 -> x7, starting transfers between devices: none -> 34.1 us  [gather_from_all(): lax.all_to_all(jnp.tile(shard, repeats), axis, split_axis=dim, concat_axi...]
    another operation x13 -> x20, local copies, waits for them, and re-layouts: 20.2 us -> 37.9 us
  transfers between devices with their start and end apart: 33 -> 33, of which waited for: 26 -> 26; matrix products, arithmetic and copies ran while one was open for 6% -> 8% of each run, Pallas kernels for 0% -> 0%
where the time goes in v1:
time: 1460 us; the launch traced here: 1450 us
  waiting for transfers between devices  1020 us (70%)
  local copies, waits for them, and re-layouts  127 us (9%)
  matrix products  119 us (8%)
  starting transfers between devices  76.8 us (5%)
  blocking collectives  46.2 us (3%)
  other arithmetic  43 us (3%)
  between operations  16 us (1%)
    reduce_scatter x7, waiting for transfers between devices, decoder_layer(): lax.psum_scatter(lax.cond(active, out_computed, out_skipped, mixed).astyp...  400 us
    all_to_all x7, waiting for transfers between devices, gather_from_all(): lax.all_to_all(jnp.tile(shard, repeats), axis, split_axis=dim, concat_axi...  318 us
    ppermute x14, waiting for transfers between devices, shifted(): return lax.ppermute(value, axis, pairs)  163 us
    all_gather x1, waiting for transfers between devices, one_gather(): lines, at, done = (lax.all_gather(flat, axis), 0, [])  66.2 us
    all_to_all x2, waiting for transfers between devices, copy_for_each(): return lax.all_to_all(copies, axis, split_axis=0, concat_axis=0, tiled=True)  59.1 us
    psum x4, blocking collectives, over_axes(): array = lax.psum(array, axis)  46.2 us
    all_to_all x7, starting transfers between devices, gather_from_all(): lax.all_to_all(jnp.tile(shard, repeats), axis, split_axis=dim, concat_axi...  34.1 us
  transfers between devices with their start and end apart: 33, of which 26 were waited for; matrix products, arithmetic and copies ran while one was open for 8% of the time, Pallas kernels for 0%

profile of v1, /device:TPU:32, one launch (start us, length us, event | category | flops | bytes accessed | tf_op | source)
XLA Modules:
  0.0 1453.9 jit_solution(8622917416079958111)
XLA Ops:
  16.4 66.2 %all-gather.3.cloned.1.call-done = bf16[7340032]{0:T(1024)(128)(2,1)} async-done(((bf16[229376]{0:T(1024)(128)(2,1)}), bf16[7340032]{0:T(1024)(128)(2,1)}) %all-gather.3.cloned.1.call-update) | async-done | bytes 14680080 | tf_op jit(solution)/shard_map/all_gather | solution.py:47
  82.6 13.3 reshape.1416
  122.5 7.9 reshape.1412
  130.4 8.2 copy.209
  141.0 27.3 %all-to-all-done = bf16[4,512,1024]{2,1,0:T(8,128)(2,1)} async-done(((bf16[4,512,1024]{2,1,0:T(8,128)(2,1)}), bf16[4,512,1024]{2,1,0:T(8,128)(2,1)}, u32[]{:S(2)}, u32[]{:S(2)}) %all-to-all-start) | async-done | bytes 4194336 | tf_op jit(solution)/shard_map/all_to_all | solution.py:31
  172.4 8.5 convolution_convert_fusion.8
  189.7 7.2 slice.282
  196.9 8.9 reshape_reshape.7
  205.8 31.9 %all-to-all-done.1 = bf16[4,512,1024]{2,1,0:T(8,128)(2,1)} async-done(((bf16[4,512,1024]{2,1,0:T(8,128)(2,1)}), bf16[4,512,1024]{2,1,0:T(8,128)(2,1)}, u32[]{:S(2)}, u32[]{:S(2)}) %all-to-all-start.1) | async-done | bytes 4194336 | tf_op jit(solution)/shard_map/all_to_all | solution.py:31
  267.1 11.7 all-to-all-done.3
  294.0 38.6 %all-to-all-done.4 = bf16[4,128,4096]{2,1,0:T(8,128)(2,1)} async-done(((bf16[4,128,4096]{2,1,0:T(8,128)(2,1)}), bf16[4,128,4096]{2,1,0:T(8,128)(2,1)}, u32[]{:S(2)}, u32[]{:S(2)}) %all-to-all-start.4) | async-done | bytes 4194336 | tf_op jit(solution)/shard_map/all_to_all | solution.py:24
  337.2 72.5 %reduce-scatter.8.cloned.1.call-done = bf16[128,4096]{1,0:T(8,128)(2,1)} async-done(((bf16[512,4096]{1,0:T(8,128)(2,1)}), bf16[128,4096]{1,0:T(8,128)(2,1)}) %reduce-scatter.8.cloned.1.call-update) | async-done | bytes 1048592 | tf_op jit(solution)/shard_map/reduce_scatter | solution.py:212
  413.7 23.3 %collective-permute-done = bf16[128,4096]{1,0:T(8,128)(2,1)S(1)} collective-permute-done((bf16[128,4096]{1,0:T(8,128)(2,1)S(1)}, bf16[128,4096]{1,0:T(8,128)(2,1)S(1)}, u32[]{:S(2)}, u32[]{:S(2)}) %collective-permute-start) | collective-permute-done | bytes 1048608 | tf_op jit(solution)/shard_map/ppermute | solution.py:58
  446.6 46.5 %all-to-all-done.5 = bf16[4,128,4096]{2,1,0:T(8,128)(2,1)} async-done(((bf16[4,128,4096]{2,1,0:T(8,128)(2,1)}), bf16[4,128,4096]{2,1,0:T(8,128)(2,1)}, u32[]{:S(2)}, u32[]{:S(2)}) %all-to-all-start.5) | async-done | bytes 4194336 | tf_op jit(solution)/shard_map/all_to_all | solution.py:24
  493.2 14.4 conditional.24
  507.6 10.5 conditional.25
  518.2 7.1 conditional.26
  518.5 6.7 fusion.357
  525.3 45.0 %reduce-scatter.10.cloned.1.call-done = bf16[128,4096]{1,0:T(8,128)(2,1)} async-done(((bf16[512,4096]{1,0:T(8,128)(2,1)}), bf16[128,4096]{1,0:T(8,128)(2,1)}) %reduce-scatter.10.cloned.1.call-update) | async-done | bytes 1048592 | tf_op jit(solution)/shard_map/reduce_scatter | solution.py:212
  573.5 23.3 %collective-permute-done.2 = bf16[128,4096]{1,0:T(8,128)(2,1)S(1)} collective-permute-done((bf16[128,4096]{1,0:T(8,128)(2,1)S(1)}, bf16[128,4096]{1,0:T(8,128)(2,1)S(1)}, u32[]{:S(2)}, u32[]{:S(2)}) %collective-permute-start.2) | collective-permute-done | bytes 1048608 | tf_op jit(solution)/shard_map/ppermute | solution.py:58
  606.5 46.5 %all-to-all-done.6 = bf16[4,128,4096]{2,1,0:T(8,128)(2,1)} async-done(((bf16[4,128,4096]{2,1,0:T(8,128)(2,1)}), bf16[4,128,4096]{2,1,0:T(8,128)(2,1)}, u32[]{:S(2)}, u32[]{:S(2)}) %all-to-all-start.6) | async-done | bytes 4194336 | tf_op jit(solution)/shard_map/all_to_all | solution.py:24
  653.0 14.4 conditional.27
  667.4 10.7 conditional.28
  678.1 6.7 conditional.29
  684.9 46.4 %reduce-scatter.12.cloned.1.call-done = bf16[128,4096]{1,0:T(8,128)(2,1)} async-done(((bf16[512,4096]{1,0:T(8,128)(2,1)}), bf16[128,4096]{1,0:T(8,128)(2,1)}) %reduce-scatter.12.cloned.1.call-update) | async-done | bytes 1048592 | tf_op jit(solution)/shard_map/reduce_scatter | solution.py:212
  734.5 23.3 %collective-permute-done.4 = bf16[128,4096]{1,0:T(8,128)(2,1)S(1)} collective-permute-done((bf16[128,4096]{1,0:T(8,128)(2,1)S(1)}, bf16[128,4096]{1,0:T(8,128)(2,1)S(1)}, u32[]{:S(2)}, u32[]{:S(2)}) %collective-permute-start.4) | collective-permute-done | bytes 1048608 | tf_op jit(solution)/shard_map/ppermute | solution.py:58
  767.5 46.5 %all-to-all-done.7 = bf16[4,128,4096]{2,1,0:T(8,128)(2,1)} async-done(((bf16[4,128,4096]{2,1,0:T(8,128)(2,1)}), bf16[4,128,4096]{2,1,0:T(8,128)(2,1)}, u32[]{:S(2)}, u32[]{:S(2)}) %all-to-all-start.7) | async-done | bytes 4194336 | tf_op jit(solution)/shard_map/all_to_all | solution.py:24
  814.0 14.6 %conditional.30 = (bf16[512,768]{0,1:T(8,128)(2,1)}) conditional(s32[]{:T(128)} %convert_element_type.543, () %tuple.154, (bf16[4,128,4096]{2,1,0:T(8,128)(2,1)}, bf16[4096,512]{0,1:T(8,128)(2,1)}, bf16[2,4096,128]{2,1,0:T(8,128)(2,1)S(1)}) %tuple.346), branch_computations={%region_44.45_spmd, %region_45.46_spmd} | conditional | flops 3226337792 | bytes 42474276 | solution.py:174
  828.6 10.5 conditional.31
  839.1 6.7 conditional.32
  845.9 46.4 %reduce-scatter.14.cloned.1.call-done = bf16[128,4096]{1,0:T(8,128)(2,1)} async-done(((bf16[512,4096]{1,0:T(8,128)(2,1)}), bf16[128,4096]{1,0:T(8,128)(2,1)}) %reduce-scatter.14.cloned.1.call-update) | async-done | bytes 1048592 | tf_op jit(solution)/shard_map/reduce_scatter | solution.py:212
  895.9 23.3 %collective-permute-done.6 = bf16[128,4096]{1,0:T(8,128)(2,1)S(1)} collective-permute-done((bf16[128,4096]{1,0:T(8,128)(2,1)S(1)}, bf16[128,4096]{1,0:T(8,128)(2,1)S(1)}, u32[]{:S(2)}, u32[]{:S(2)}) %collective-permute-start.6) | collective-permute-done | bytes 1048608 | tf_op jit(solution)/shard_map/ppermute | solution.py:58
  928.9 46.5 %all-to-all-done.8 = bf16[4,128,4096]{2,1,0:T(8,128)(2,1)} async-done(((bf16[4,128,4096]{2,1,0:T(8,128)(2,1)}), bf16[4,128,4096]{2,1,0:T(8,128)(2,1)}, u32[]{:S(2)}, u32[]{:S(2)}) %all-to-all-start.8) | async-done | bytes 4194336 | tf_op jit(solution)/shard_map/all_to_all | solution.py:24
  975.4 14.4 conditional.33
  989.8 10.5 conditional.34
  1000.4 6.9 conditional.35
  1000.5 6.7 fusion.360
  1007.3 46.5 %reduce-scatter.16.cloned.1.call-done = bf16[128,4096]{1,0:T(8,128)(2,1)} async-done(((bf16[512,4096]{1,0:T(8,128)(2,1)}), bf16[128,4096]{1,0:T(8,128)(2,1)}) %reduce-scatter.16.cloned.1.call-update) | async-done | bytes 1048592 | tf_op jit(solution)/shard_map/reduce_scatter | solution.py:212
  1056.9 23.3 %collective-permute-done.8 = bf16[128,4096]{1,0:T(8,128)(2,1)S(1)} collective-permute-done((bf16[128,4096]{1,0:T(8,128)(2,1)S(1)}, bf16[128,4096]{1,0:T(8,128)(2,1)S(1)}, u32[]{:S(2)}, u32[]{:S(2)}) %collective-permute-start.8) | collective-permute-done | bytes 1048608 | tf_op jit(solution)/shard_map/ppermute | solution.py:58
  1089.9 46.5 %all-to-all-done.9 = bf16[4,128,4096]{2,1,0:T(8,128)(2,1)} async-done(((bf16[4,128,4096]{2,1,0:T(8,128)(2,1)}), bf16[4,128,4096]{2,1,0:T(8,128)(2,1)}, u32[]{:S(2)}, u32[]{:S(2)}) %all-to-all-start.9) | async-done | bytes 4194336 | tf_op jit(solution)/shard_map/all_to_all | solution.py:24
  1141.0 73.8 %reduce-scatter.18.cloned.1.call-done = bf16[128,4096]{1,0:T(8,128)(2,1)} async-done(((bf16[512,4096]{1,0:T(8,128)(2,1)}), bf16[128,4096]{1,0:T(8,128)(2,1)}) %reduce-scatter.18.cloned.1.call-update) | async-done | bytes 1048592 | tf_op jit(solution)/shard_map/reduce_scatter | solution.py:212
  1217.9 23.3 %collective-permute-done.10 = bf16[128,4096]{1,0:T(8,128)(2,1)S(1)} collective-permute-done((bf16[128,4096]{1,0:T(8,128)(2,1)S(1)}, bf16[128,4096]{1,0:T(8,128)(2,1)S(1)}, u32[]{:S(2)}, u32[]{:S(2)}) %collective-permute-start.10) | collective-permute-done | bytes 1048608 | tf_op jit(solution)/shard_map/ppermute | solution.py:58
  1250.9 46.5 %all-to-all-done.10 = bf16[4,128,4096]{2,1,0:T(8,128)(2,1)} async-done(((bf16[4,128,4096]{2,1,0:T(8,128)(2,1)}), bf16[4,128,4096]{2,1,0:T(8,128)(2,1)}, u32[]{:S(2)}, u32[]{:S(2)}) %all-to-all-start.10) | async-done | bytes 4194336 | tf_op jit(solution)/shard_map/all_to_all | solution.py:24
  1300.3 69.3 %reduce-scatter.20.cloned.1.call-done = bf16[128,4096]{1,0:T(8,128)(2,1)} async-done(((bf16[512,4096]{1,0:T(8,128)(2,1)}), bf16[128,4096]{1,0:T(8,128)(2,1)}) %reduce-scatter.20.cloned.1.call-update) | async-done | bytes 1048592 | tf_op jit(solution)/shard_map/reduce_scatter | solution.py:212
  1372.8 23.3 %collective-permute-done.12 = bf16[128,4096]{1,0:T(8,128)(2,1)S(1)} collective-permute-done((bf16[128,4096]{1,0:T(8,128)(2,1)S(1)}, bf16[128,4096]{1,0:T(8,128)(2,1)S(1)}, u32[]{:S(2)}, u32[]{:S(2)}) %collective-permute-start.12) | collective-permute-done | bytes 1048608 | tf_op jit(solution)/shard_map/ppermute | solution.py:58
  1398.3 26.3 %psum.28 = s32[]{:T(128)} all-reduce(s32[]{:T(128)} %reduce_sum.242), channel_id=1, replica_groups=mesh['section'=4,'dp_0'=4,'dp_1'=2,'mp'=4] {'section'}, use_global_device_ids=true, to_apply=%region_84.85 | all-reduce | flops 1 | bytes 8 | tf_op jit(solution)/shard_map/psum | solution.py:63
  1424.6 9.5 psum.29
  1436.5 8.0 psum.31
  (287 shorter events, 319.0 us)
Async XLA Ops:
  7.2 7.3 copy-start.1
  7.2 7.7 copy-start.17
  7.2 7.8 copy-start.18
  7.2 75.4 %all-gather.3.cloned.1.call-start = ((), (), s32[]{:S(2)}) async-start(), calls=%async_computation.25 | async-start | bytes 15138816 | tf_op jit(solution)/shard_map/all_gather | solution.py:47
  113.7 54.6 %all-to-all-start = ((bf16[4,512,1024]{2,1,0:T(8,128)(2,1)}), bf16[4,512,1024]{2,1,0:T(8,128)(2,1)}, u32[]{:S(2)}, u32[]{:S(2)}) async-start(bf16[4,512,1024]{2,1,0:T(8,128)(2,1)} %broadcast_in_dim.76), calls=%async_computation | async-start | bytes 8388608 | tf_op jit(solution)/shard_map/all_to_all | solution.py:31
  130.4 8.2 copy-start.4
  183.6 5.4 copy-start.20
  183.6 54.1 %all-to-all-start.1 = ((bf16[4,512,1024]{2,1,0:T(8,128)(2,1)}), bf16[4,512,1024]{2,1,0:T(8,128)(2,1)}, u32[]{:S(2)}, u32[]{:S(2)}) async-start(bf16[4,512,1024]{2,1,0:T(8,128)(2,1)} %broadcast_in_dim.85), calls=%async_computation.1 | async-start | bytes 8388608 | tf_op jit(solution)/shard_map/all_to_all | solution.py:31
  243.6 10.8 copy-start.19
  249.3 16.8 %copy-start.2 = (bf16[1,128,4096]{2,1,0:T(8,128)(2,1)S(1)}, bf16[1,128,4096]{2,1,0:T(8,128)(2,1)}, u32[]{:S(2)}) copy-start(bf16[1,128,4096]{2,1,0:T(8,128)(2,1)} %param.59) | copy-start | bytes 3145732
  249.3 11.7 all-to-all-start.2
  262.5 17.0 %copy-start.14 = (f32[1,4096]{1,0:T(1,128)S(1)}, f32[1,4096]{1,0:T(1,128)}, u32[]{:S(2)}) copy-start(f32[1,4096]{1,0:T(1,128)} %param.65) | copy-start | bytes 49156
  262.5 16.3 %all-to-all-start.3 = ((bf16[4,128,1024]{2,1,0:T(8,128)(2,1)}), bf16[4,128,1024]{2,1,0:T(8,128)(2,1)S(1)}, u32[]{:S(2)}, u32[]{:S(2)}) async-start(bf16[4,128,1024]{2,1,0:T(8,128)(2,1)} %bitcast.156), calls=%async_computation.3 | async-start | bytes 2097152 | tf_op jit(solution)/shard_map/all_to_all | solution.py:297
  279.4 3.1 copy-start.3
  282.5 50.1 %all-to-all-start.4 = ((bf16[4,128,4096]{2,1,0:T(8,128)(2,1)}), bf16[4,128,4096]{2,1,0:T(8,128)(2,1)}, u32[]{:S(2)}, u32[]{:S(2)}) async-start(bf16[4,128,4096]{2,1,0:T(8,128)(2,1)} %tile.14), calls=%async_computation.4 | async-start | bytes 8388608 | tf_op jit(solution)/shard_map/all_to_all | solution.py:24
  287.4 122.3 %reduce-scatter.8.cloned.1.call-start = ((), (), s32[]{:S(2)}) async-start(), calls=%async_computation.18 | async-start | bytes 5242880 | tf_op jit(solution)/shard_map/reduce_scatter | solution.py:212
  287.4 45.2 %copy-start = (bf16[1,2,4096,128]{3,2,1,0:T(8,128)(2,1)S(1)}, bf16[1,2,4096,128]{3,2,1,0:T(8,128)(2,1)}, u32[]{:S(2)}) copy-start(bf16[1,2,4096,128]{3,2,1,0:T(8,128)(2,1)} %param.67) | copy-start | bytes 6291460
  411.8 25.1 %collective-permute-start = (bf16[128,4096]{1,0:T(8,128)(2,1)S(1)}, bf16[128,4096]{1,0:T(8,128)(2,1)S(1)}, u32[]{:S(2)}, u32[]{:S(2)}) collective-permute-start(bf16[128,4096]{1,0:T(8,128)(2,1)S(1)} %fusion.241), channel_id=1, source_target_pairs={{0,32},{32,64},{64,96},{96,0},{1,33},{33,65},{65,97},{97,1},{2,34}... | collective-permute-start | bytes 3145736 | tf_op jit(solution)/shard_map/ppermute | solution.py:58
  440.1 53.1 %all-to-all-start.5 = ((bf16[4,128,4096]{2,1,0:T(8,128)(2,1)}), bf16[4,128,4096]{2,1,0:T(8,128)(2,1)}, u32[]{:S(2)}, u32[]{:S(2)}) async-start(bf16[4,128,4096]{2,1,0:T(8,128)(2,1)} %tile.15), calls=%async_computation.6 | async-start | bytes 8388608 | tf_op jit(solution)/shard_map/all_to_all | solution.py:24
  445.0 125.4 %reduce-scatter.10.cloned.1.call-start = ((), (), s32[]{:S(2)}) async-start(), calls=%async_computation.19 | async-start | bytes 5242880 | tf_op jit(solution)/shard_map/reduce_scatter | solution.py:212
  445.0 62.6 %collective-permute-start.1 = (s32[512]{0:T(512)S(1)}, s32[512]{0:T(512)S(1)}, u32[]{:S(2)}, u32[]{:S(2)}) collective-permute-start(s32[512]{0:T(512)S(1)} %bitcast.579), channel_id=1, source_target_pairs={{0,32},{32,64},{64,96},{96,0},{1,33},{33,65},{65,97},{97,1},{2,34}... | collective-permute-start | bytes 6152 | tf_op jit(solution)/shard_map/ppermute | solution.py:58
  496.9 4.5 copy-start.6
  571.9 24.9 %collective-permute-start.2 = (bf16[128,4096]{1,0:T(8,128)(2,1)S(1)}, bf16[128,4096]{1,0:T(8,128)(2,1)S(1)}, u32[]{:S(2)}, u32[]{:S(2)}) collective-permute-start(bf16[128,4096]{1,0:T(8,128)(2,1)S(1)} %fusion.240), channel_id=1, source_target_pairs={{0,32},{32,64},{64,96},{96,0},{1,33},{33,65},{65,97},{97,1},{2,34}... | collective-permute-start | bytes 3145736 | tf_op jit(solution)/shard_map/ppermute | solution.py:58
  599.9 53.1 %all-to-all-start.6 = ((bf16[4,128,4096]{2,1,0:T(8,128)(2,1)}), bf16[4,128,4096]{2,1,0:T(8,128)(2,1)}, u32[]{:S(2)}, u32[]{:S(2)}) async-start(bf16[4,128,4096]{2,1,0:T(8,128)(2,1)} %tile.16), calls=%async_computation.8 | async-start | bytes 8388608 | tf_op jit(solution)/shard_map/all_to_all | solution.py:24
  604.8 126.5 %reduce-scatter.12.cloned.1.call-start = ((), (), s32[]{:S(2)}) async-start(), calls=%async_computation.20 | async-start | bytes 5242880 | tf_op jit(solution)/shard_map/reduce_scatter | solution.py:212
  604.8 62.6 %collective-permute-start.3 = (s32[512]{0:T(512)S(1)}, s32[512]{0:T(512)S(1)}, u32[]{:S(2)}, u32[]{:S(2)}) collective-permute-start(s32[512]{0:T(512)S(1)} %collective-permute-done.1), channel_id=1, source_target_pairs={{0,32},{32,64},{64,96},{96,0},{1,33},{33,65},{65,97},{97,1},{2,34}... | collective-permute-start | bytes 6152 | tf_op jit(solution)/shard_map/ppermute | solution.py:58
  656.7 4.5 copy-start.7
  732.8 24.9 %collective-permute-start.4 = (bf16[128,4096]{1,0:T(8,128)(2,1)S(1)}, bf16[128,4096]{1,0:T(8,128)(2,1)S(1)}, u32[]{:S(2)}, u32[]{:S(2)}) collective-permute-start(bf16[128,4096]{1,0:T(8,128)(2,1)S(1)} %fusion.239), channel_id=1, source_target_pairs={{0,32},{32,64},{64,96},{96,0},{1,33},{33,65},{65,97},{97,1},{2,34}... | collective-permute-start | bytes 3145736 | tf_op jit(solution)/shard_map/ppermute | solution.py:58
  760.9 53.1 %all-to-all-start.7 = ((bf16[4,128,4096]{2,1,0:T(8,128)(2,1)}), bf16[4,128,4096]{2,1,0:T(8,128)(2,1)}, u32[]{:S(2)}, u32[]{:S(2)}) async-start(bf16[4,128,4096]{2,1,0:T(8,128)(2,1)} %tile.17), calls=%async_computation.10 | async-start | bytes 8388608 | tf_op jit(solution)/shard_map/all_to_all | solution.py:24
  765.8 126.6 %reduce-scatter.14.cloned.1.call-start = ((), (), s32[]{:S(2)}) async-start(), calls=%async_computation.21 | async-start | bytes 5242880 | tf_op jit(solution)/shard_map/reduce_scatter | solution.py:212
  765.8 62.8 %collective-permute-start.5 = (s32[512]{0:T(512)S(1)}, s32[512]{0:T(512)S(1)}, u32[]{:S(2)}, u32[]{:S(2)}) collective-permute-start(s32[512]{0:T(512)S(1)} %collective-permute-done.3), channel_id=1, source_target_pairs={{0,32},{32,64},{64,96},{96,0},{1,33},{33,65},{65,97},{97,1},{2,34}... | collective-permute-start | bytes 6152 | tf_op jit(solution)/shard_map/ppermute | solution.py:58
  817.9 4.5 copy-start.8
  893.9 25.3 %collective-permute-start.6 = (bf16[128,4096]{1,0:T(8,128)(2,1)S(1)}, bf16[128,4096]{1,0:T(8,128)(2,1)S(1)}, u32[]{:S(2)}, u32[]{:S(2)}) collective-permute-start(bf16[128,4096]{1,0:T(8,128)(2,1)S(1)} %fusion.238), channel_id=1, source_target_pairs={{0,32},{32,64},{64,96},{96,0},{1,33},{33,65},{65,97},{97,1},{2,34}... | collective-permute-start | bytes 3145736 | tf_op jit(solution)/shard_map/ppermute | solution.py:58
  922.3 53.1 %all-to-all-start.8 = ((bf16[4,128,4096]{2,1,0:T(8,128)(2,1)}), bf16[4,128,4096]{2,1,0:T(8,128)(2,1)}, u32[]{:S(2)}, u32[]{:S(2)}) async-start(bf16[4,128,4096]{2,1,0:T(8,128)(2,1)} %tile.18), calls=%async_computation.12 | async-start | bytes 8388608 | tf_op jit(solution)/shard_map/all_to_all | solution.py:24
  927.2 126.6 %reduce-scatter.16.cloned.1.call-start = ((), (), s32[]{:S(2)}) async-start(), calls=%async_computation.22 | async-start | bytes 5242880 | tf_op jit(solution)/shard_map/reduce_scatter | solution.py:212
  927.3 62.6 %collective-permute-start.7 = (s32[512]{0:T(512)S(1)}, s32[512]{0:T(512)S(1)}, u32[]{:S(2)}, u32[]{:S(2)}) collective-permute-start(s32[512]{0:T(512)S(1)} %collective-permute-done.5), channel_id=1, source_target_pairs={{0,32},{32,64},{64,96},{96,0},{1,33},{33,65},{65,97},{97,1},{2,34}... | collective-permute-start | bytes 6152 | tf_op jit(solution)/shard_map/ppermute | solution.py:58
  979.1 4.5 copy-start.9
  1055.3 24.9 %collective-permute-start.8 = (bf16[128,4096]{1,0:T(8,128)(2,1)S(1)}, bf16[128,4096]{1,0:T(8,128)(2,1)S(1)}, u32[]{:S(2)}, u32[]{:S(2)}) collective-permute-start(bf16[128,4096]{1,0:T(8,128)(2,1)S(1)} %fusion.237), channel_id=1, source_target_pairs={{0,32},{32,64},{64,96},{96,0},{1,33},{33,65},{65,97},{97,1},{2,34}... | collective-permute-start | bytes 3145736 | tf_op jit(solution)/shard_map/ppermute | solution.py:58
  1083.3 53.1 %all-to-all-start.9 = ((bf16[4,128,4096]{2,1,0:T(8,128)(2,1)}), bf16[4,128,4096]{2,1,0:T(8,128)(2,1)}, u32[]{:S(2)}, u32[]{:S(2)}) async-start(bf16[4,128,4096]{2,1,0:T(8,128)(2,1)} %tile.19), calls=%async_computation.14 | async-start | bytes 8388608 | tf_op jit(solution)/shard_map/all_to_all | solution.py:24
  1088.2 126.6 %reduce-scatter.18.cloned.1.call-start = ((), (), s32[]{:S(2)}) async-start(), calls=%async_computation.23 | async-start | bytes 5242880 | tf_op jit(solution)/shard_map/reduce_scatter | solution.py:212
  1088.3 49.1 %collective-permute-start.9 = (s32[512]{0:T(512)S(1)}, s32[512]{0:T(512)S(1)}, u32[]{:S(2)}, u32[]{:S(2)}) collective-permute-start(s32[512]{0:T(512)S(1)} %collective-permute-done.7), channel_id=1, source_target_pairs={{0,32},{32,64},{64,96},{96,0},{1,33},{33,65},{65,97},{97,1},{2,34}... | collective-permute-start | bytes 6152 | tf_op jit(solution)/shard_map/ppermute | solution.py:58
  1216.3 24.9 %collective-permute-start.10 = (bf16[128,4096]{1,0:T(8,128)(2,1)S(1)}, bf16[128,4096]{1,0:T(8,128)(2,1)S(1)}, u32[]{:S(2)}, u32[]{:S(2)}) collective-permute-start(bf16[128,4096]{1,0:T(8,128)(2,1)S(1)} %fusion.236), channel_id=1, source_target_pairs={{0,32},{32,64},{64,96},{96,0},{1,33},{33,65},{65,97},{97,1},{2,34}... | collective-permute-start | bytes 3145736 | tf_op jit(solution)/shard_map/ppermute | solution.py:58
  1244.4 53.1 %all-to-all-start.10 = ((bf16[4,128,4096]{2,1,0:T(8,128)(2,1)}), bf16[4,128,4096]{2,1,0:T(8,128)(2,1)}, u32[]{:S(2)}, u32[]{:S(2)}) async-start(bf16[4,128,4096]{2,1,0:T(8,128)(2,1)} %tile.20), calls=%async_computation.16 | async-start | bytes 8388608 | tf_op jit(solution)/shard_map/all_to_all | solution.py:24
  1249.2 120.4 %reduce-scatter.20.cloned.1.call-start = ((), (), s32[]{:S(2)}) async-start(), calls=%async_computation.24 | async-start | bytes 5242880 | tf_op jit(solution)/shard_map/reduce_scatter | solution.py:212
  1249.3 48.5 %collective-permute-start.11 = (s32[512]{0:T(512)S(1)}, s32[512]{0:T(512)S(1)}, u32[]{:S(2)}, u32[]{:S(2)}) collective-permute-start(s32[512]{0:T(512)S(1)} %collective-permute-done.9), channel_id=1, source_target_pairs={{0,32},{32,64},{64,96},{96,0},{1,33},{33,65},{65,97},{97,1},{2,34}... | collective-permute-start | bytes 6152 | tf_op jit(solution)/shard_map/ppermute | solution.py:58
  1300.3 97.3 %copy-start.21 = (s32[1,128]{1,0:T(1,128)S(1)}, s32[1,128]{1,0:T(1,128)}, u32[]{:S(2)}) copy-start(s32[1,128]{1,0:T(1,128)} %param.62) | copy-start | bytes 1540
  1371.2 24.9 %collective-permute-start.12 = (bf16[128,4096]{1,0:T(8,128)(2,1)S(1)}, bf16[128,4096]{1,0:T(8,128)(2,1)S(1)}, u32[]{:S(2)}, u32[]{:S(2)}) collective-permute-start(bf16[128,4096]{1,0:T(8,128)(2,1)S(1)} %fusion.235), channel_id=1, source_target_pairs={{0,32},{32,64},{64,96},{96,0},{1,33},{33,65},{65,97},{97,1},{2,34}... | collective-permute-start | bytes 3145736 | tf_op jit(solution)/shard_map/ppermute | solution.py:58
  1396.1 49.6 %collective-permute-start.13 = (bf16[128,4096]{1,0:T(8,128)(2,1)S(1)}, bf16[128,4096]{1,0:T(8,128)(2,1)S(1)}, u32[]{:S(2)}, u32[]{:S(2)}) collective-permute-start(bf16[128,4096]{1,0:T(8,128)(2,1)S(1)} %collective-permute-done.12), channel_id=1, source_target_pairs={{0,32},{32,64},{64,96},{96,0},{1,33},{33,65},{65,97},{97,1},{2,34}... | collective-permute-start | bytes 3145736 | tf_op jit(solution)/shard_map/ppermute | solution.py:58
  (6 other events, 10.0 us)
Sparse Core Ops, SparseCore 0:
  13.2 69.3 all-gather.2
  337.3 72.3 reduce-scatter.7
  525.4 44.8 reduce-scatter.9
  685.0 46.2 reduce-scatter.11
  846.0 46.2 reduce-scatter.13
  1007.4 46.2 reduce-scatter.15
  1141.1 73.6 reduce-scatter.17
  1300.4 69.1 reduce-scatter.19
